TPU v7x, 32 devices: a whole 2x2x4 slice. The times are simulated.
32 devices in a mesh: range: 16 (over z, x, core), dop: 2 (over y).
Axes of the slice: x: 2, y: 2, z: 4, core: 2. Of those that a mesh axis runs over, the one named last changes fastest.
Arguments:
- echoes: float32 [2, 128, 16, 8192], P(None, None, None, ('range', 'dop')), may hold values from -200 to 200
- triplet: int32 [128, 3], replicated, may hold values from 0 to 127, as said below
- bin_taper: float32 [128, 3], replicated, may hold values from 0.2 to 1
- phases: float32 [16], replicated, may hold values from -3.140625 to 3.140625
- excluded: int32 [128, 512], P('dop', 'range'), may hold values 0 or 1
- guard_len: int32 [128], P('dop'), may hold values from 1 to 4, as said below
- train_len: int32 [128], P('dop'), may hold values from 32 to 64, as said below
Outputs:
- cfar_ratio: float32 [128, 8192], P('dop', 'range')
Inputs may be any that keep to these rules, and one draw needn't show every extreme that they name: `triplet`: row b holds a bin below b, b itself, and a bin above b, each within 2 of b counted cyclically over 128 bins. `guard_len`: some bin has exactly 4. `train_len`: some bin has exactly 64.
All inputs are finite; a program needn't handle non-finite values. No bound on the sum of `excluded` on one device may be relied on, other than what follows from the above.
Results may differ from a plain program's by a relative error of at most 0.0003.
Values sent between devices are 32-bit elements; how exact they have to be, the bound alone decides.
A program may use at most 64 MiB of HBM per device.

v0:
```python
import jax
import jax.numpy as jnp
from jax import lax
from jax.sharding import PartitionSpec as P

BLOCK = 16
GUARD_MAX = 4
TRAIN_MAX = 64


full_precision = lax.Precision.HIGHEST
epsilon = 1e-06


def extended(block, sides, width):
    for axis, dim in sides:
        count = lax.axis_size(axis)
        forward = [(i, i + 1) for i in range(count - 1)]
        backward = [(target, source) for source, target in forward]
        low = lax.ppermute(
            lax.slice_in_dim(block, block.shape[dim] - width, None, axis=dim), axis, forward
        )
        high = lax.ppermute(lax.slice_in_dim(block, 0, width, axis=dim), axis, backward)
        block = jnp.concatenate([low, block, high], axis=dim)
    return block


def gram_blocks(snapshot, kept_mask):
    snap_real = snapshot[0]
    snap_imag = snapshot[1]
    kept_real = snap_real * kept_mask[:, None, :]
    kept_imag = snap_imag * kept_mask[:, None, :]
    cov_real = jnp.einsum(
        "bir,bjr->bij", kept_real, snap_real, precision=full_precision
    ) + jnp.einsum("bir,bjr->bij", kept_imag, snap_imag, precision=full_precision)
    cov_imag = jnp.einsum(
        "bir,bjr->bij", kept_imag, snap_real, precision=full_precision
    ) - jnp.einsum("bir,bjr->bij", kept_real, snap_imag, precision=full_precision)
    bin_count = snapshot.shape[1]
    space_time = snapshot.shape[2]
    return jnp.concatenate([cov_real, cov_imag], axis=1).reshape(
        bin_count, 2 * space_time * space_time
    )


def solve_system(gram_term, taper_rows, phases, total_range):
    bin_count = gram_term.shape[0]
    space_time = taper_rows.shape[1] * phases.shape[0]
    blocks = gram_term.reshape(bin_count, 2, space_time, space_time)
    real_part = blocks[:, 0]
    imag_part = blocks[:, 1]
    system = (
        jnp.concatenate(
            [
                jnp.concatenate([real_part, -imag_part], axis=2),
                jnp.concatenate([imag_part, real_part], axis=2),
            ],
            axis=1,
        )
        / total_range
    )
    cosines = (taper_rows[:, :, None] * jnp.cos(phases)[None, None, :]).reshape(
        bin_count, space_time
    )
    sines = (taper_rows[:, :, None] * jnp.sin(phases)[None, None, :]).reshape(bin_count, space_time)
    right_side = jnp.concatenate([cosines, sines], axis=1)[:, :, None]
    factor = jnp.linalg.cholesky(system)
    halfway = lax.linalg.triangular_solve(factor, right_side, left_side=True, lower=True)
    solved = lax.linalg.triangular_solve(
        factor, halfway, left_side=True, lower=True, transpose_a=True
    )
    return solved[:, :, 0]


def apply_weights(snapshot, weights):
    space_time = snapshot.shape[2]
    weight_real = weights[:, :space_time]
    weight_imag = weights[:, space_time:]
    real_out = jnp.einsum(
        "bi,bir->br", weight_real, snapshot[0], precision=full_precision
    ) + jnp.einsum("bi,bir->br", weight_imag, snapshot[1], precision=full_precision)
    imag_out = jnp.einsum(
        "bi,bir->br", weight_real, snapshot[1], precision=full_precision
    ) - jnp.einsum("bi,bir->br", weight_imag, snapshot[0], precision=full_precision)
    return real_out * real_out + imag_out * imag_out


def form_snapshot(padded_bins, bin_rows, bin_total):
    bin_count = bin_rows.shape[0]
    centre_ids = jnp.arange(bin_count, dtype=jnp.int32)
    offset_rows = jnp.mod(bin_rows - centre_ids[:, None], bin_total)
    slot_list = []
    for slot in range(bin_rows.shape[1]):
        chosen = padded_bins[:, 2 : 2 + bin_count]
        for offset in (-2, -1, 1, 2):
            matches = (offset_rows[:, slot] == offset % bin_total)[None, :, None, None]
            chosen = jnp.where(matches, padded_bins[:, 2 + offset : 2 + offset + bin_count], chosen)
        slot_list.append(chosen)
    stacked = jnp.stack(slot_list, axis=2)
    return stacked.reshape(
        2, bin_count, bin_rows.shape[1] * padded_bins.shape[2], padded_bins.shape[3]
    )


def wrap_bins(echoes):
    return jnp.concatenate([echoes[:, -2:], echoes, echoes[:, :2]], axis=1)


def detect(power_map, padded, guard_len, train_len, gate_start, total_range, reach_len):
    cell_total = power_map.shape[1]
    cell_ids = jnp.arange(cell_total, dtype=jnp.int32)[None, :]
    guard_col = guard_len[:, None]
    train_col = train_len[:, None]
    window_sum = jnp.zeros(power_map.shape, jnp.float32)
    for offset in range(1, reach_len + 1):
        inside = jnp.logical_and(guard_col < offset, offset <= guard_col + train_col).astype(
            jnp.float32
        )
        both_sides = (
            padded[:, reach_len - offset : reach_len - offset + cell_total]
            + padded[:, reach_len + offset : reach_len + offset + cell_total]
        )
        window_sum = window_sum + inside * both_sides
    position = gate_start + cell_ids
    left_count = jnp.maximum(
        jnp.minimum(position - guard_col - 1, total_range - 1)
        - jnp.maximum(position - guard_col - train_col, 0)
        + 1,
        0,
    )
    right_count = jnp.maximum(
        jnp.minimum(position + guard_col + train_col, total_range - 1)
        - jnp.maximum(position + guard_col + 1, 0)
        + 1,
        0,
    )
    noise_level = window_sum / (left_count + right_count).astype(jnp.float32)
    return power_map / (noise_level + epsilon)


def shards(echoes, triplet, bin_taper, phases, excluded, guard_len, train_len):
    bin_total = echoes.shape[1]
    range_count = lax.axis_size("range")
    range_rank = lax.axis_index("range")
    dop_rank = lax.axis_index("dop")
    bin_dev = excluded.shape[0]
    range_dev = excluded.shape[1] * BLOCK
    total_range = range_dev * range_count
    stacked = form_snapshot(wrap_bins(echoes), triplet, bin_total)
    bin_major = lax.all_to_all(stacked, "dop", split_axis=1, concat_axis=3, tiled=True)
    kept_mask = (1 - jnp.repeat(excluded, BLOCK, axis=1)).astype(jnp.float32)
    share_count = bin_dev // range_count
    own_gram = lax.psum_scatter(
        gram_blocks(bin_major, kept_mask), "range", scatter_dimension=0, tiled=True
    )
    first_bin = dop_rank * bin_dev + range_rank * share_count
    own_weights = solve_system(
        own_gram,
        lax.dynamic_slice_in_dim(bin_taper, first_bin, share_count, 0),
        phases,
        total_range,
    )
    weights = lax.all_gather(own_weights, "range", axis=0, tiled=True)
    power_map = apply_weights(bin_major, weights)
    reach_len = GUARD_MAX + TRAIN_MAX
    padded = extended(power_map, (("range", 1),), reach_len)
    return detect(
        power_map, padded, guard_len, train_len, range_rank * range_dev, total_range, reach_len
    )


def solution(mesh):
    placed = (
        P(None, None, None, ("range", "dop")),
        P(),
        P(),
        P(),
        P("dop", "range"),
        P("dop"),
        P("dop"),
    )
    return jax.shard_map(
        shards, mesh=mesh, in_specs=placed, out_specs=P("dop", "range"), check_vma=False
    )
```

profile of v0, /device:TPU:0, one launch (start us, length us, event | category | flops | bytes accessed | tf_op | source)
XLA Modules:
  0.0 502.3 jit_solution(9210021970062562865)
XLA Ops:
  8.2 9.6 %fusion.17 = f32[2,128,1,16,256]{4,3,2,1,0:T(8,128)S(1)} fusion(f32[2,128,16,256]{3,2,1,0:T(8,128)} %param.7, f32[2,2,16,256]{3,2,1,0:T(8,128)S(1)} %get-tuple-element.10, f32[2,2,16,256]{3,2,1,0:T(8,128)S(1)} %get-tuple-element.9, pred[128]{0:T(512)(128)(4,1)S(1)} %get-tuple-element.20, pred[128]{0:T(512)(128)(4,1)S(1)} %get-tuple-element.19, ...), kind=kLoop, calls=%fused_computation.25 | loop fusion | flops 8388608 | bytes 8520192 | tf_op jit(solution)/shard_map/stack | solution.py:99
  23.3 5.1 %pad_maximum_fusion = f32[2,128,3,16,256]{4,3,2,1,0:T(8,128)} fusion(f32[2,128,1,16,256]{4,3,2,1,0:T(8,128)S(1)} %fusion.13, f32[2,128,1,16,256]{4,3,2,1,0:T(8,128)S(1)} %fusion.21, f32[2,128,1,16,256]{4,3,2,1,0:T(8,128)S(1)} %fusion.17), kind=kLoop, calls=%fused_computation | loop fusion | flops 6291456 | bytes 25165824 | tf_op jit(solution)/shard_map/stack | solution.py:99
  28.4 10.9 %copy.35 = f32[2,128,48,256]{3,2,0,1:T(8,128)} copy(f32[2,128,48,256]{3,2,1,0:T(8,128)} %bitcast.109) | data formatting | bytes 25165824 | tf_op jit(solution)/shard_map/reshape | solution.py:100
  39.3 8.5 %all-to-all-start = ((f32[2,128,48,256]{3,2,0,1:T(8,128)}), f32[2,128,48,256]{3,2,0,1:T(8,128)}, u32[]{:S(2)}, u32[]{:S(2)}) async-start(f32[2,128,48,256]{3,2,0,1:T(8,128)} %copy.35), calls=%async_computation | async-start | bytes 25165824 | tf_op jit(solution)/shard_map/all_to_all | solution.py:150
  48.8 137.8 %all-to-all-done = f32[2,128,48,256]{3,2,0,1:T(8,128)} async-done(((f32[2,128,48,256]{3,2,0,1:T(8,128)}), f32[2,128,48,256]{3,2,0,1:T(8,128)}, u32[]{:S(2)}, u32[]{:S(2)}) %all-to-all-start) | async-done | bytes 12582944 | tf_op jit(solution)/shard_map/all_to_all | solution.py:150
  186.6 10.6 %copy.36 = f32[2,128,48,256]{3,2,1,0:T(8,128)} copy(f32[2,128,48,256]{3,2,0,1:T(8,128)} %all-to-all-done) | data formatting | bytes 25165824 | tf_op jit(solution)/shard_map/all_to_all | solution.py:150
  197.2 8.5 %fusion.392 = (f32[1,64,48,2,256]{4,2,1,3,0:T(8,128)S(1)}, f32[1,64,48,2,256]{4,2,1,3,0:T(8,128)}) fusion(f32[2,64,48,2,256]{4,2,1,3,0:T(8,128)} %bitcast.110), kind=kLoop, calls=%fused_computation.773 | loop fusion | bytes 25165824 | tf_op jit(solution)/shard_map/slice | solution.py:30
  205.7 8.3 %copy.39 = f32[1,64,48,2,256]{4,3,2,1,0:T(2,128)} copy(f32[1,64,48,2,256]{4,2,1,3,0:T(8,128)S(1)} %get-tuple-element.7) | data formatting | bytes 12582912 | tf_op jit(solution)/shard_map/slice | solution.py:30
  214.0 9.2 %squeeze.9 = f32[64,48,512]{2,1,0:T(8,128)} reshape(f32[1,64,48,2,256]{4,3,2,1,0:T(2,128)} %copy.39) | data formatting | bytes 12582912 | tf_op jit(solution)/shard_map/squeeze | solution.py:30
  223.1 11.1 %copy.37 = f32[1,64,48,2,256]{4,3,2,1,0:T(2,128)} copy(f32[1,64,48,2,256]{4,2,1,3,0:T(8,128)} %get-tuple-element.8) | data formatting | bytes 12582912 | tf_op jit(solution)/shard_map/slice | solution.py:29
  234.2 9.1 %squeeze.8 = f32[64,48,512]{2,1,0:T(8,128)} reshape(f32[1,64,48,2,256]{4,3,2,1,0:T(2,128)} %copy.37) | data formatting | bytes 12582912 | tf_op jit(solution)/shard_map/squeeze | solution.py:29
  243.3 11.4 %fusion.2 = f32[64,48,48]{1,2,0:T(8,128)S(1)} fusion(f32[64,48,512]{2,1,0:T(8,128)} %squeeze.9, f32[64,512]{1,0:T(8,128)S(1)} %copy.38), kind=kOutput, calls=%fused_computation.3 | convolution fusion | flops 907542528 | bytes 7012352 | tf_op jit(solution)/shard_map/bir,bjr->bij/dot_general | solution.py:35
  254.8 7.0 %fusion = f32[64,48,48]{1,2,0:T(8,128)S(1)} fusion(f32[64,48,512]{2,1,0:T(8,128)S(1)} %copy-done.2, f32[64,48,512]{2,1,0:T(8,128)S(1)} %bitcast.104, f32[64,512]{1,0:T(8,128)S(1)} %copy.38), kind=kOutput, calls=%fused_computation.1 | convolution fusion | flops 907542528 | bytes 13303808 | tf_op jit(solution)/shard_map/bir,bjr->bij/dot_general | solution.py:36
  261.8 7.1 %fusion.26 = f32[64,48,48]{1,2,0:T(8,128)S(1)} fusion(f32[64,48,48]{1,2,0:T(8,128)S(1)} %fusion.2, f32[64,48,512]{2,1,0:T(8,128)S(1)} %copy-done.2, f32[64,512]{1,0:T(8,128)S(1)} %copy.38), kind=kOutput, calls=%fused_computation.170 | convolution fusion | flops 907689984 | bytes 7602176 | tf_op jit(solution)/shard_map/bir,bjr->bij/dot_general | solution.py:33
  268.9 7.1 %fusion.29 = f32[64,48,48]{1,2,0:T(8,128)S(1)} fusion(f32[64,48,48]{1,2,0:T(8,128)S(1)} %fusion, f32[64,48,512]{2,1,0:T(8,128)S(1)} %bitcast.104, f32[64,48,512]{2,1,0:T(8,128)S(1)} %copy-done.2, f32[64,512]{1,0:T(8,128)S(1)} %copy.38), kind=kOutput, calls=%fused_computation.171 | convolution fusion | flops 907689984 | bytes 13893632 | tf_op jit(solution)/shard_map/bir,bjr->bij/dot_general | solution.py:38
  284.3 93.3 %all-reduce.3.cloned.1.call-done = f32[64,4608]{1,0:T(8,128)} async-done(((f32[64,4608]{1,0:T(8,128)}), f32[64,4608]{1,0:T(8,128)}) %all-reduce.3.cloned.1.call-update) | async-done | bytes 1179664
  379.3 35.2 %custom-call.9 = f32[4,96,96]{2,1,0:T(8,128)S(1)} custom-call(f32[4,96,96]{2,1,0:T(8,128)S(1)} %fusion.35), custom_call_target="Cholesky" | custom-call | tf_op jit(solution)/shard_map/jit(cholesky)/cholesky | solution.py:67
  414.8 29.5 %custom-call.10 = f32[4,1,96,96]{2,3,1,0:T(8,128)S(1)} custom-call(f32[4,1,96,96]{3,2,1,0:T(8,128)S(1)} %select_bitcast_fusion), custom_call_target="InvertDiagBlocksLowerTriangular" | custom-call | tf_op jit(solution)/shard_map/triangular_solve | solution.py:69
  445.0 19.4 %all-gather = f32[16,4,96]{2,1,0:T(4,128)S(1)} all-gather(f32[1,4,96]{2,1,0:T(4,128)S(1)} %bitcast.122), channel_id=1, replica_groups=mesh['range'=16,'dop'=2] {'range'}, dimensions={0}, use_global_device_ids=true | all-gather | bytes 26112 | tf_op jit(solution)/shard_map/all_gather | solution.py:163
  464.5 5.5 %fusion.398 = f32[64,1,512]{2,1,0:T(1,128)S(1)} fusion(f32[64,48,1]{1,2,0:T(1,128)S(1)} %bitcast.118, f32[64,48,512]{2,1,0:T(8,128)} %squeeze.8), kind=kOutput, calls=%fused_computation.779 | convolution fusion | flops 18874368 | bytes 6434816 | tf_op jit(solution)/shard_map/bi,bir->br/dot_general | solution.py:79
  470.0 5.3 %fusion.400 = f32[64,1,512]{2,1,0:T(1,128)S(1)} fusion(f32[64,48,1]{1,2,0:T(1,128)S(1)} %bitcast.119, f32[64,48,512]{2,1,0:T(8,128)} %squeeze.9), kind=kOutput, calls=%fused_computation.781 | convolution fusion | flops 18874368 | bytes 6434816 | tf_op jit(solution)/shard_map/bi,bir->br/dot_general | solution.py:82
  475.3 3.1 fusion.399
  478.5 3.1 fusion.401
  487.0 8.1 %fusion.50 = f32[64,512]{1,0:T(8,128)} fusion(f32[64,512]{1,0:T(8,128)S(1)} %fusion.389, f32[64,68]{1,0:T(8,128)S(1)} %collective-permute-done.1, f32[64,68]{1,0:T(8,128)S(1)} %collective-permute-done, s32[64]{0:T(128)S(1)} %copy-done.6, s32[64]{0:T(128)S(1)} %copy-done.5, s32[512]{0:T(512)S(1)} %iota_add_fusion, f32[64]{0:T(128)S(1)} %get-tuple-element.97, ...), kind=kLoop, calls=%fused_computation.333 | loop fusion | flops 11796480 | bytes 316928 | tf_op jit(solution)/shard_map/div | solution.py:138
  (84 shorter events, 23.7 us)
Async XLA Ops:
  6.5 41.7 %copy-start = (f32[128,3]{0,1:T(4,128)S(1)}, f32[128,3]{0,1:T(4,128)}, u32[]{:S(2)}) copy-start(f32[128,3]{0,1:T(4,128)} %param.9) | copy-start | bytes 4612
  8.1 9.7 %copy-start.3 = (f32[2,128,16,256]{3,2,1,0:T(8,128)S(1)}, f32[2,128,16,256]{3,2,1,0:T(8,128)}, u32[]{:S(2)}) copy-start(f32[2,128,16,256]{3,2,1,0:T(8,128)} %param.7) | copy-start | bytes 12582916
  39.3 8.7 %copy-start.4 = (s32[64,32]{0,1:T(8,128)S(1)}, s32[64,32]{0,1:T(8,128)}, u32[]{:S(2)}) copy-start(s32[64,32]{0,1:T(8,128)} %param.11) | copy-start | bytes 24580
  39.3 9.3 %copy-start.7 = (f32[16]{0:T(128)S(1)}, f32[16]{0:T(128)}, u32[]{:S(2)}) copy-start(f32[16]{0:T(128)} %param.10) | copy-start | bytes 196
  39.3 147.3 %all-to-all-start = ((f32[2,128,48,256]{3,2,0,1:T(8,128)}), f32[2,128,48,256]{3,2,0,1:T(8,128)}, u32[]{:S(2)}, u32[]{:S(2)}) async-start(f32[2,128,48,256]{3,2,0,1:T(8,128)} %copy.35), calls=%async_computation | async-start | bytes 25165824 | tf_op jit(solution)/shard_map/all_to_all | solution.py:150
  47.8 329.8 %all-reduce.3.cloned.1.call-start = ((), (), s32[]{:S(2)}) async-start(), calls=%async_computation.1 | async-start | bytes 2359296
  234.2 20.6 %slice-start = ((s8[6291456]{0:T(1024)(128)(4,1)}), s8[2097152]{0:T(1024)(128)(4,1)S(1)}, s32[]{:S(2)}) async-start(s8[6291456]{0:T(1024)(128)(4,1)} %bitcast.103), calls=%async_computation.2 | async-start | bytes 4194304
  243.3 11.5 %slice-start.1 = ((s8[6291456]{0:T(1024)(128)(4,1)}), s8[4194304]{0:T(1024)(128)(4,1)S(1)}, s32[]{:S(2)}) async-start(s8[6291456]{0:T(1024)(128)(4,1)} %bitcast.103), calls=%async_computation.3 | async-start | bytes 8388608
  243.3 11.5 %copy-start.2 = (f32[64,48,512]{2,1,0:T(8,128)S(1)}, f32[64,48,512]{2,1,0:T(8,128)}, u32[]{:S(2)}) copy-start(f32[64,48,512]{2,1,0:T(8,128)} %squeeze.8) | copy-start | bytes 18874372
  277.6 5.4 %copy-start.8 = (u32[32]{0:T(128)S(1)}, u32[32]{0:T(128)}, u32[]{:S(2)}) copy-start(u32[32]{0:T(128)} %constant.229) | copy-start | bytes 388
  277.6 6.6 %copy-start.5 = (s32[64]{0:T(128)S(1)}, s32[64]{0:T(128)}, u32[]{:S(2)}) copy-start(s32[64]{0:T(128)} %param.12) | copy-start | bytes 772
  277.6 6.6 %copy-start.6 = (s32[64]{0:T(128)S(1)}, s32[64]{0:T(128)}, u32[]{:S(2)}) copy-start(s32[64]{0:T(128)} %param.13) | copy-start | bytes 772
  414.5 60.8 %slice-start.2 = ((s8[6291456]{0:T(1024)(128)(4,1)}), s8[2097152]{0:T(1024)(128)(4,1)S(1)}, s32[]{:S(2)}) async-start(s8[6291456]{0:T(1024)(128)(4,1)} %bitcast.105), calls=%async_computation.4 | async-start | bytes 4194304
  464.5 10.8 %slice-start.3 = ((s8[6291456]{0:T(1024)(128)(4,1)}), s8[4194304]{0:T(1024)(128)(4,1)S(1)}, s32[]{:S(2)}) async-start(s8[6291456]{0:T(1024)(128)(4,1)} %bitcast.105), calls=%async_computation.5 | async-start | bytes 8388608
  464.5 14.0 %slice-start.4 = ((s8[6291456]{0:T(1024)(128)(4,1)}), s8[4194304]{0:T(1024)(128)(4,1)S(1)}, s32[]{:S(2)}) async-start(s8[6291456]{0:T(1024)(128)(4,1)} %bitcast.107), calls=%async_computation.6 | async-start | bytes 8388608
  470.0 8.5 %slice-start.5 = ((s8[6291456]{0:T(1024)(128)(4,1)}), s8[2097152]{0:T(1024)(128)(4,1)S(1)}, s32[]{:S(2)}) async-start(s8[6291456]{0:T(1024)(128)(4,1)} %bitcast.107), calls=%async_computation.7 | async-start | bytes 4194304
  475.3 19.9 %copy-start.1 = (f32[128,3]{0,1:T(4,128)S(1)}, f32[128,3]{0,1:T(4,128)}, u32[]{:S(2)}) copy-start(f32[128,3]{0,1:T(4,128)} %param.9) | copy-start | bytes 4612
  481.7 3.6 collective-permute-start
  483.9 3.1 collective-permute-start.1
Sparse Core Ops, SparseCore 0:
  283.0 94.6 all-reduce.2
where the time goes:
time: 509 us; the launch traced here: 502 us
  waiting for transfers between devices  233 us (46%)
  other arithmetic  96.1 us (19%)
  local copies, waits for them, and re-layouts  76.6 us (15%)
  matrix products  50.2 us (10%)
  blocking collectives  19.4 us (4%)
  between operations  14.7 us (3%)
  starting transfers between devices  12.2 us (2%)
    all_to_all x1, waiting for transfers between devices, shards(): lax.all_to_all(stacked, 'dop', split_axis=1, concat_axis=3, tiled=True)  138 us
    unnamed x2, waiting for transfers between devices  93.4 us
    another operation x4, other arithmetic, solve_system(): factor = jnp.linalg.cholesky(system)  35.4 us
    another operation x3, other arithmetic, solve_system(): lax.linalg.triangular_solve(factor, halfway, left_side=True, lower=True,...  29.6 us
    another operation x4, other arithmetic, form_snapshot(): stacked = jnp.stack(slot_list, axis=2)  20.2 us
    all_gather x1, blocking collectives, shards(): weights = lax.all_gather(own_weights, 'range', axis=0, tiled=True)  19.4 us
    slice x2, local copies, waits for them, and re-layouts, gram_blocks(): snap_imag = snapshot[1]  16.7 us
    dot_general x1, matrix products, gram_blocks(): jnp.einsum('bir,bjr->bij', kept_imag, snap_imag, precision=full_precision)  11.4 us
  transfers between devices with their start and end apart: 4, of which 3 were waited for; matrix products, arithmetic and copies ran while one was open for 0% of the time, Pallas kernels for 0%

commit v1 on v0

v1 whole, which is shorter than its diff:
```python
import functools

import jax
import jax.numpy as jnp
from jax import lax
from jax.experimental import pallas as pl
from jax.experimental.pallas import tpu as pltpu
from jax.sharding import PartitionSpec as P

BLOCK = 16
GUARD_MAX = 4
TRAIN_MAX = 64
LANES = 128
epsilon = 1e-06

MESH = pl.DeviceIdType.MESH
VMEM = pl.BlockSpec(memory_space=pltpu.VMEM)
SMEM = pl.BlockSpec(memory_space=pltpu.SMEM)
VMEM_LIMIT = 60 * 1024 * 1024


def grid_sizes(range_count, dop_count):
    core = 2 if range_count % 2 == 0 else 1
    rest = range_count // core
    near = 1
    while near * near * 4 <= rest and rest % (near * 2) == 0:
        near *= 2
    return core, dop_count, near, rest // near


def place_of(sizes, index):
    core, dops, near, far = sizes
    c = index // (dops * near * far)
    y = (index // (near * far)) % dops
    x = (index // far) % near
    z = index % far
    return ((z * near + x) * core + c, y)


def my_parts(sizes):
    core, _, near, _ = sizes
    r = lax.axis_index("range")
    return r % core, lax.axis_index("dop"), (r // core) % near, r // (core * near)


def chunk_index(sizes, parts):
    core, dops, near, far = sizes
    c, y, x, z = parts
    return ((c * dops + y) * near + x) * far + z


def greet(devices):
    barrier = pltpu.get_barrier_semaphore()
    for device in devices:
        pl.semaphore_signal(barrier, inc=1, device_id=device, device_id_type=MESH)
    pl.semaphore_wait(barrier, len(devices))


def mask_kernel(dops, excl_ref, out_ref, send_sems, recv_sems, local_sem):
    r = lax.axis_index("range")
    y = lax.axis_index("dop")
    greet([(r, (y + k) % dops) for k in range(1, dops)])
    copies = []
    for k in range(1, dops):
        copies.append(
            pltpu.make_async_remote_copy(
                src_ref=excl_ref,
                dst_ref=out_ref.at[y],
                send_sem=send_sems.at[k - 1],
                recv_sem=recv_sems.at[k - 1],
                device_id=(r, (y + k) % dops),
                device_id_type=MESH,
            )
        )
        copies[-1].start()
    own = pltpu.make_async_copy(excl_ref, out_ref.at[y], local_sem)
    own.start()
    own.wait()
    for copy in copies:
        copy.wait()


def gather_mask(excluded, dops):
    bins, blocks = excluded.shape
    if dops == 1:
        return excluded
    gathered = pl.pallas_call(
        functools.partial(mask_kernel, dops),
        out_shape=jax.ShapeDtypeStruct((dops, bins, blocks), jnp.int32),
        in_specs=[VMEM],
        out_specs=VMEM,
        scratch_shapes=[
            pltpu.SemaphoreType.DMA((dops - 1,)),
            pltpu.SemaphoreType.DMA((dops - 1,)),
            pltpu.SemaphoreType.DMA,
        ],
        compiler_params=pltpu.CompilerParams(collective_id=0, has_side_effects=True),
    )(excluded)
    return gathered.reshape(dops * bins, blocks)


def gram_kernel(trip_ref, echo_ref, excl_ref, out_ref, kept_ref):
    slots = trip_ref.shape[1]
    chans, gates = echo_ref.shape[2:]
    span = slots * chans
    blocks = excl_ref.shape[1]
    first = lax.axis_index("dop") * (gates // BLOCK)
    block_ids = lax.broadcasted_iota(jnp.int32, (blocks, gates), 0)
    gate_blocks = lax.broadcasted_iota(jnp.int32, (blocks, gates), 1) // BLOCK + first
    spread = jnp.where(block_ids == gate_blocks, 1.0, 0.0).astype(jnp.bfloat16)
    kept_ref[...] = 1.0 - jnp.dot(
        excl_ref[...].astype(jnp.float32).astype(jnp.bfloat16),
        spread,
        preferred_element_type=jnp.float32,
    )
    rows = lax.broadcasted_iota(jnp.int32, (span, LANES), 0)
    lanes = lax.broadcasted_iota(jnp.int32, (span, LANES), 1)
    upper_even = rows <= lanes
    upper_odd = rows <= lanes - span
    is_even = lanes < span
    filler = jnp.zeros((LANES - 2 * span, 8 * gates), jnp.bfloat16)

    def split(values):
        high = values.astype(jnp.bfloat16)
        return high, (values - high.astype(jnp.float32)).astype(jnp.bfloat16)

    def pair_step(pair, carry):
        lefts = []
        rights = []
        for s in range(2):
            b = 2 * pair + s
            u = jnp.concatenate([echo_ref[0, trip_ref[b, t]] for t in range(slots)], axis=0)
            v = jnp.concatenate([echo_ref[1, trip_ref[b, t]] for t in range(slots)], axis=0)
            kept = kept_ref[pl.ds(b, 1), :].astype(jnp.bfloat16)
            uh, ul = split(u)
            vh, vl = split(v)
            uhm, ulm, vhm, vlm = uh * kept, ul * kept, vh * kept, vl * kept
            rights.append(jnp.concatenate([uh, vh, uh, vh, ul, vl, ul, vl], axis=1))
            lefts.append(jnp.concatenate([uhm, vhm, ulm, vlm] * 2, axis=1))
            lefts.append(jnp.concatenate([vhm, -uhm, vlm, -ulm] * 2, axis=1))
        left = jnp.concatenate(lefts, axis=0)
        right = jnp.concatenate(rights + [filler], axis=0)
        product = lax.dot_general(
            left, right, (((1,), (1,)), ((), ())), preferred_element_type=jnp.float32
        )
        even = jnp.where(upper_even, product[:span], product[span : 2 * span])
        odd = jnp.where(upper_odd, product[2 * span : 3 * span], product[3 * span :])
        out_ref[pair] = jnp.where(is_even, even, odd)
        return carry

    lax.fori_loop(0, out_ref.shape[0], pair_step, 0)


def gram(triplet, echoes, excl_all):
    bins, slots = triplet.shape
    chans, gates = echoes.shape[2:]
    return pl.pallas_call(
        gram_kernel,
        out_shape=jax.ShapeDtypeStruct((bins // 2, slots * chans, LANES), jnp.float32),
        in_specs=[SMEM, VMEM, VMEM],
        out_specs=VMEM,
        scratch_shapes=[pltpu.VMEM((bins, gates), jnp.float32)],
        compiler_params=pltpu.CompilerParams(vmem_limit_bytes=VMEM_LIMIT),
    )(triplet, echoes, excl_all)


def reduce_plan(sizes, total_rows, span):
    count = sizes[0] * sizes[1] * sizes[2] * sizes[3]
    split_core = (total_rows // span) % count == 0
    plan = []
    rows = total_rows
    for axis, group in enumerate(sizes):
        if group == 1:
            continue
        after = rows if axis == 0 and not split_core else rows // group
        plan.append((axis, group, rows, after))
        rows = after
    return plan, rows


def reduce_kernel(sizes, plan, part_ref, out_ref, *scratch):
    phases = len(plan)
    recv_bufs = scratch[:phases]
    sums = scratch[phases : 2 * phases - 1]
    send_sems, recv_sems = scratch[2 * phases - 1 :]
    parts = my_parts(sizes)

    def peer(axis, group, k):
        moved = list(parts)
        moved[axis] = (parts[axis] + k) % group
        return moved[axis], place_of(sizes, chunk_index(sizes, moved))

    greet([peer(axis, group, k)[1] for axis, group, _, _ in plan for k in range(1, group)])
    current = part_ref
    sem = 0
    for phase, (axis, group, before, after) in enumerate(plan):
        whole = before == after
        copies = []
        for k in range(1, group):
            where, device = peer(axis, group, k)
            start = 0 if whole else pl.multiple_of(where * after, 8)
            copies.append(
                pltpu.make_async_remote_copy(
                    src_ref=current.at[pl.ds(start, after)],
                    dst_ref=recv_bufs[phase].at[k - 1],
                    send_sem=send_sems.at[sem],
                    recv_sem=recv_sems.at[sem],
                    device_id=device,
                    device_id_type=MESH,
                )
            )
            copies[-1].start()
            sem += 1
        own = 0 if whole else pl.multiple_of(parts[axis] * after, 8)
        for copy in copies:
            copy.wait()
        total = current[pl.ds(own, after), :]
        for k in range(1, group):
            total = total + recv_bufs[phase][k - 1]
        if phase == phases - 1:
            out_ref[...] = total
        else:
            sums[phase][...] = total
            current = sums[phase]


def reduce_grams(partial, sizes, span):
    total_rows = partial.shape[0]
    plan, rows = reduce_plan(sizes, total_rows, span)
    copies = sum(group - 1 for _, group, _, _ in plan)
    return pl.pallas_call(
        functools.partial(reduce_kernel, sizes, plan),
        out_shape=jax.ShapeDtypeStruct((rows, LANES), jnp.float32),
        in_specs=[VMEM],
        out_specs=VMEM,
        scratch_shapes=[
            pltpu.VMEM((group - 1, after, LANES), jnp.float32) for _, group, _, after in plan
        ]
        + [pltpu.VMEM((after, LANES), jnp.float32) for _, _, _, after in plan[:-1]]
        + [pltpu.SemaphoreType.DMA((copies,)), pltpu.SemaphoreType.DMA((copies,))],
        compiler_params=pltpu.CompilerParams(
            collective_id=1, has_side_effects=True, vmem_limit_bytes=VMEM_LIMIT
        ),
    )(partial)


def solve_kernel(total_range, gram_ref, right_ref, out_ref):
    span = right_ref.shape[1]
    pairs = gram_ref.shape[0] // span
    rows = lax.broadcasted_iota(jnp.int32, (span, LANES), 0)
    lanes = lax.broadcasted_iota(jnp.int32, (span, LANES), 1)
    scale = 1.0 / total_range
    systems = []
    for pair in range(pairs):
        packed = gram_ref[pair * span : (pair + 1) * span, :] * scale
        padded = jnp.concatenate(
            [packed, jnp.zeros((LANES - span, LANES), jnp.float32)], axis=0
        )
        turned = padded.T
        for s in range(2):
            here = packed if s == 0 else pltpu.roll(packed, LANES - span, axis=1)
            there = turned[s * span : (s + 1) * span, :]
            real = jnp.where(rows <= lanes, here, there)
            imag = jnp.where(rows > lanes, here, jnp.where(rows < lanes, -there, 0.0))
            b = 2 * pair + s
            real = jnp.where(lanes < span, real, jnp.where(lanes == span, right_ref[2 * b], 0.0))
            imag = jnp.where(
                lanes < span, imag, jnp.where(lanes == span, right_ref[2 * b + 1], 0.0)
            )
            systems.append((real, imag))
    for k in range(span):
        for b, (real, imag) in enumerate(systems):
            inverse = 1.0 / real[k : k + 1, k : k + 1]
            row_real = real[k : k + 1, :] * inverse
            row_imag = imag[k : k + 1, :] * inverse
            col_real = real[:, k : k + 1]
            col_imag = imag[:, k : k + 1]
            pivot = rows == k
            next_real = jnp.where(
                pivot, row_real, real - (col_real * row_real - col_imag * row_imag)
            )
            next_imag = jnp.where(
                pivot, row_imag, imag - (col_real * row_imag + col_imag * row_real)
            )
            systems[b] = (next_real, next_imag)
    columns = jnp.zeros((span, LANES), jnp.float32)
    for b, (real, imag) in enumerate(systems):
        columns = jnp.where(lanes == 2 * b, real[:, span : span + 1], columns)
        columns = jnp.where(lanes == 2 * b + 1, imag[:, span : span + 1], columns)
    padded = jnp.concatenate([columns, jnp.zeros((LANES - span, LANES), jnp.float32)], axis=0)
    out_ref[...] = padded.T[: out_ref.shape[0], :]


def solve(own_gram, right, total_range):
    held = -(-right.shape[0] // 8) * 8
    return pl.pallas_call(
        functools.partial(solve_kernel, total_range),
        out_shape=jax.ShapeDtypeStruct((held, LANES), jnp.float32),
        in_specs=[VMEM, VMEM],
        out_specs=VMEM,
    )(own_gram, right)


def weights_kernel(sizes, own_ref, out_ref, send_sems, recv_sems, local_sem):
    count = out_ref.shape[0]
    me = chunk_index(sizes, my_parts(sizes))
    devices = [place_of(sizes, (me + k) % count) for k in range(1, count)]
    greet(devices)
    copies = []
    for k, device in enumerate(devices):
        copies.append(
            pltpu.make_async_remote_copy(
                src_ref=own_ref,
                dst_ref=out_ref.at[me],
                send_sem=send_sems.at[k],
                recv_sem=recv_sems.at[k],
                device_id=device,
                device_id_type=MESH,
            )
        )
        copies[-1].start()
    own = pltpu.make_async_copy(own_ref, out_ref.at[me], local_sem)
    own.start()
    own.wait()
    for copy in copies:
        copy.wait()


def gather_weights(own, sizes):
    count = sizes[0] * sizes[1] * sizes[2] * sizes[3]
    return pl.pallas_call(
        functools.partial(weights_kernel, sizes),
        out_shape=jax.ShapeDtypeStruct((count,) + own.shape, jnp.float32),
        in_specs=[VMEM],
        out_specs=VMEM,
        scratch_shapes=[
            pltpu.SemaphoreType.DMA((count - 1,)),
            pltpu.SemaphoreType.DMA((count - 1,)),
            pltpu.SemaphoreType.DMA,
        ],
        compiler_params=pltpu.CompilerParams(collective_id=2, has_side_effects=True),
    )(own)


def power_kernel(owned, trip_ref, echo_ref, weight_ref, out_ref, turned_ref):
    slots = trip_ref.shape[1]
    held = weight_ref.shape[1]
    span = turned_ref.shape[1]
    owners = trip_ref.shape[0] // owned
    per_tile = LANES // held
    for tile in range(turned_ref.shape[0]):
        block = weight_ref[tile * per_tile : (tile + 1) * per_tile].reshape(LANES, LANES)
        turned_ref[tile] = block.T[:span, :]

    def owner_step(owner, carry):
        shift = (owner % per_tile) * held
        rolled = pltpu.roll(turned_ref[owner // per_tile], (LANES - shift) % LANES, axis=1)
        for k in range(owned):
            b = owner * owned + k
            wr = rolled[:, 2 * k : 2 * k + 1]
            wi = rolled[:, 2 * k + 1 : 2 * k + 2]
            u = jnp.concatenate([echo_ref[0, trip_ref[b, t]] for t in range(slots)], axis=0)
            v = jnp.concatenate([echo_ref[1, trip_ref[b, t]] for t in range(slots)], axis=0)
            yr = jnp.sum(wr * u + wi * v, axis=0, keepdims=True)
            yi = jnp.sum(wr * v - wi * u, axis=0, keepdims=True)
            out_ref[pl.ds(b, 1), :] = yr * yr + yi * yi
        return carry

    lax.fori_loop(0, owners, owner_step, 0)


def apply_weights(triplet, echoes, weights, owned):
    bins, slots = triplet.shape
    chans, gates = echoes.shape[2:]
    tiles = (bins // owned) * weights.shape[1] // LANES
    return pl.pallas_call(
        functools.partial(power_kernel, owned),
        out_shape=jax.ShapeDtypeStruct((bins, gates), jnp.float32),
        in_specs=[SMEM, VMEM, VMEM],
        out_specs=VMEM,
        scratch_shapes=[pltpu.VMEM((tiles, slots * chans, LANES), jnp.float32)],
        compiler_params=pltpu.CompilerParams(vmem_limit_bytes=VMEM_LIMIT),
    )(triplet, echoes, weights)


def exchange_kernel(sizes, power_ref, out_ref, send_sems, recv_sems, local_sem):
    dops = sizes[1]
    ranges = sizes[0] * sizes[2] * sizes[3]
    bins = out_ref.shape[0]
    gates = power_ref.shape[1]
    r = lax.axis_index("range")
    y = lax.axis_index("dop")
    last = ranges - 1
    left_row = (r + last) % ranges
    right_row = (r + 1) % ranges
    greet(
        [(r, (y + k) % dops) for k in range(1, dops)]
        + [(left_row, k) for k in range(dops)]
        + [(right_row, k) for k in range(dops)]
    )
    middle = LANES + pl.multiple_of(y * gates, LANES)
    copies = []
    for k in range(1, dops):
        target = (y + k) % dops
        copies.append(
            pltpu.make_async_remote_copy(
                src_ref=power_ref.at[pl.ds(pl.multiple_of(target * bins, 8), bins), :],
                dst_ref=out_ref.at[:, pl.ds(middle, gates)],
                send_sem=send_sems.at[k - 1],
                recv_sem=recv_sems.at[k - 1],
                device_id=(r, target),
                device_id_type=MESH,
            )
        )
        copies[-1].start()

    def halo(k, to_right):
        source = gates - LANES if to_right else 0
        target = LANES + dops * gates if not to_right else 0
        number = dops - 1 + k + (dops if to_right else 0)
        return pltpu.make_async_remote_copy(
            src_ref=power_ref.at[k * bins : (k + 1) * bins, source : source + LANES],
            dst_ref=out_ref.at[:, target : target + LANES],
            send_sem=send_sems.at[number],
            recv_sem=recv_sems.at[dops - 1 + (1 if to_right else 0)],
            device_id=(right_row if to_right else left_row, k),
            device_id_type=MESH,
        )

    sends_right = jnp.logical_and(y == dops - 1, r < last)
    sends_left = jnp.logical_and(y == 0, r > 0)

    @pl.when(sends_right)
    def _():
        for k in range(dops):
            halo(k, True).start()

    @pl.when(sends_left)
    def _():
        for k in range(dops):
            halo(k, False).start()

    own = pltpu.make_async_copy(
        power_ref.at[pl.ds(pl.multiple_of(y * bins, 8), bins), :],
        out_ref.at[:, pl.ds(middle, gates)],
        local_sem,
    )
    own.start()

    @pl.when(r == 0)
    def _():
        out_ref[:, :LANES] = jnp.zeros((bins, LANES), jnp.float32)

    @pl.when(r == last)
    def _():
        out_ref[:, LANES + dops * gates :] = jnp.zeros((bins, LANES), jnp.float32)

    own.wait()
    for copy in copies:
        copy.wait()

    @pl.when(sends_right)
    def _():
        for k in range(dops):
            halo(k, True).wait_send()

    @pl.when(sends_left)
    def _():
        for k in range(dops):
            halo(k, False).wait_send()

    @pl.when(r > 0)
    def _():
        halo(0, True).wait_recv()

    @pl.when(r < last)
    def _():
        halo(0, False).wait_recv()


def exchange_power(power, sizes):
    bins, gates = power.shape
    dops = sizes[1]
    return pl.pallas_call(
        functools.partial(exchange_kernel, sizes),
        out_shape=jax.ShapeDtypeStruct((bins // dops, dops * gates + 2 * LANES), jnp.float32),
        in_specs=[VMEM],
        out_specs=VMEM,
        scratch_shapes=[
            pltpu.SemaphoreType.DMA((3 * dops - 1,)),
            pltpu.SemaphoreType.DMA((dops + 1,)),
            pltpu.SemaphoreType.DMA,
        ],
        compiler_params=pltpu.CompilerParams(collective_id=3, has_side_effects=True),
    )(power)


def detect_kernel(total_range, padded_ref, guard_ref, train_ref, out_ref):
    width = padded_ref.shape[1]
    cells = out_ref.shape[1]
    padded = padded_ref[...]
    guard = guard_ref[...]
    train = train_ref[...]

    def ahead(values, by):
        return pltpu.roll(values, (width - by) % width, axis=1)

    def behind(values, by):
        return pltpu.roll(values, by % width, axis=1)

    forward = padded
    right = jnp.zeros_like(padded)
    left = jnp.zeros_like(padded)
    step = 1
    while step <= TRAIN_MAX:
        chosen = (train & step) != 0
        backward = behind(forward, step - 1) if step > 1 else forward
        right = jnp.where(chosen, forward + ahead(right, step), right)
        left = jnp.where(chosen, backward + behind(left, step), left)
        forward = forward + ahead(forward, step)
        step *= 2
    total = jnp.zeros_like(padded)
    for size in range(1, GUARD_MAX + 1):
        both = ahead(right, size + 1) + behind(left, size + 1)
        total = jnp.where(guard == size, both, total)
    start = lax.axis_index("range") * cells
    position = start + lax.broadcasted_iota(jnp.int32, (out_ref.shape[0], cells), 1)
    left_count = jnp.maximum(
        jnp.minimum(position - guard - 1, total_range - 1)
        - jnp.maximum(position - guard - train, 0)
        + 1,
        0,
    )
    right_count = jnp.maximum(
        jnp.minimum(position + guard + train, total_range - 1)
        - jnp.maximum(position + guard + 1, 0)
        + 1,
        0,
    )
    noise = total[:, LANES : LANES + cells] / (left_count + right_count).astype(jnp.float32)
    out_ref[...] = padded[:, LANES : LANES + cells] / (noise + epsilon)


def detect(padded, guard_len, train_len, total_range):
    bins, width = padded.shape
    return pl.pallas_call(
        functools.partial(detect_kernel, total_range),
        out_shape=jax.ShapeDtypeStruct((bins, width - 2 * LANES), jnp.float32),
        in_specs=[VMEM, VMEM, VMEM],
        out_specs=VMEM,
    )(padded, guard_len[:, None], train_len[:, None])


def shards(echoes, triplet, bin_taper, phases, excluded, guard_len, train_len):
    bins, slots = triplet.shape
    chans = echoes.shape[2]
    span = slots * chans
    ranges = lax.axis_size("range")
    dops = lax.axis_size("dop")
    sizes = grid_sizes(ranges, dops)
    total_range = excluded.shape[1] * BLOCK * ranges
    partial = gram(triplet, echoes, gather_mask(excluded, dops))
    own_gram = reduce_grams(partial.reshape(bins // 2 * span, LANES), sizes, span)
    owned = own_gram.shape[0] // span * 2
    owner = chunk_index(sizes, my_parts(sizes)) % (bins // owned)
    taper = lax.dynamic_slice_in_dim(bin_taper, owner * owned, owned, 0)
    turns = jnp.stack([jnp.cos(phases), jnp.sin(phases)])
    right = (taper[:, None, :, None] * turns[None, :, None, :]).reshape(2 * owned, span, 1)
    own_weights = solve(own_gram, right, total_range)
    weights = gather_weights(own_weights, sizes)
    power = apply_weights(triplet, echoes, weights, owned)
    padded = exchange_power(power, sizes)
    return detect(padded, guard_len, train_len, total_range)


def solution(mesh):
    placed = (
        P(None, None, None, ("range", "dop")),
        P(),
        P(),
        P(),
        P("dop", "range"),
        P("dop"),
        P("dop"),
    )
    return jax.shard_map(
        shards, mesh=mesh, in_specs=placed, out_specs=P("dop", "range"), check_vma=False
    )
```

time: 509 us -> 109 us (0.21); the launches traced: 502 us -> 109 us
  waiting for transfers between devices: 233 us -> 0 us
  Pallas kernels: 0 us -> 103 us
  other arithmetic: 96.1 us -> 0.09 us
  local copies, waits for them, and re-layouts: 76.6 us -> 5.3 us
  matrix products: 50.2 us -> 0 us
  blocking collectives: 19.4 us -> 0 us
  between operations: 14.7 us -> 0.13 us
  starting transfers between devices: 12.2 us -> 0 us
    all_to_all x1 -> x0, waiting for transfers between devices: 138 us -> none  [shards(): lax.all_to_all(stacked, 'dop', split_axis=1, concat_axis=3, tiled=True)]
    pallas_call x0 -> x8, Pallas kernels: none -> 103 us  [the longest x1 30 us: reduce_grams(): pl.pallas_call(functools.partial(reduce_kernel, sizes, plan), out_shape=j...]
    unnamed x2 -> x0, waiting for transfers between devices: 93.4 us -> none
    another operation x11 -> x1, other arithmetic: 85.1 us -> 0.01 us  [shards(): turns = jnp.stack([jnp.cos(phases), jnp.sin(phases)])]
    dot_general x8 -> x0, matrix products: 49.5 us -> none  [the longest x1 11.4 us: gram_blocks(): jnp.einsum('bir,bjr->bij', kept_imag, snap_imag, precision=full_precision)]
    slice x7 -> x0, local copies, waits for them, and re-layouts: 28.9 us -> none  [the longest x2 16.7 us: gram_blocks(): snap_imag = snapshot[1]]
    all_gather x1 -> x0, blocking collectives: 19.4 us -> none  [shards(): weights = lax.all_gather(own_weights, 'range', axis=0, tiled=True)]
    squeeze x2 -> x0, local copies, waits for them, and re-layouts: 18.3 us -> none  [the longest x1 9.16 us: gram_blocks(): snap_imag = snapshot[1]]
  transfers between devices with their start and end apart: 4 -> 0, of which waited for: 3 -> 0; matrix products, arithmetic and copies ran while one was open for 0% -> 0% of each run, Pallas kernels for 0% -> 0%
where the time goes in v1:
time: 109 us
  Pallas kernels  103 us (94%)
  local copies, waits for them, and re-layouts  5.3 us (5%)
    pallas_call x1, Pallas kernels, reduce_grams(): pl.pallas_call(functools.partial(reduce_kernel, sizes, plan), out_shape=j...  30 us
    pallas_call x1, Pallas kernels, gram(): pl.pallas_call(gram_kernel, out_shape=jax.ShapeDtypeStruct((bins // 2, sl...  27 us
    pallas_call x1, Pallas kernels, gather_weights(): pl.pallas_call(functools.partial(weights_kernel, sizes), out_shape=jax.Sh...  11.1 us
    pallas_call x1, Pallas kernels, apply_weights(): pl.pallas_call(functools.partial(power_kernel, owned), out_shape=jax.Shap...  10.3 us
    pallas_call x1, Pallas kernels, solve(): pl.pallas_call(functools.partial(solve_kernel, total_range), out_shape=ja...  7.61 us
    pallas_call x1, Pallas kernels, exchange_power(): pl.pallas_call(functools.partial(exchange_kernel, sizes), out_shape=jax.S...  7.31 us
    pallas_call x1, Pallas kernels, gather_mask(): pl.pallas_call(functools.partial(mask_kernel, dops), out_shape=jax.ShapeD...  6.29 us
    pallas_call x1, Pallas kernels, detect(): pl.pallas_call(functools.partial(detect_kernel, total_range), out_shape=j...  3.66 us

profile of v1, /device:TPU:0, one launch (start us, length us, event | category | flops | bytes accessed | tf_op | source)
XLA Modules:
  0.0 108.8 jit_solution(6855802292992665937)
XLA Ops:
  0.0 0.0 copy-start
  0.0 0.0 copy-start.3
  0.0 1.4 %copy.18.trip_ref = s32[128,3]{1,0:T(8,128)} copy(s32[128,3]{0,1:T(4,128)} %param.8) | data formatting | bytes 3072 | tf_op args[1]
  1.4 1.4 %copy.14.excl_ref = s32[64,32]{1,0:T(8,128)} copy(s32[64,32]{0,1:T(8,128)} %param.11) | data formatting | bytes 16384 | tf_op args[4]
  2.9 6.3 %shard_map.73 = s32[2,64,32]{2,1,0:T(8,128)} custom-call(s32[64,32]{1,0:T(8,128)} %copy.14.excl_ref), custom_call_target="tpu_custom_call" | custom-call | tf_op jit(solution)/shard_map/pallas_call | solution.py:87
  9.1 27.0 %shard_map.74 = f32[64,48,128]{2,1,0:T(8,128)} custom-call(s32[128,3]{1,0:T(8,128)} %copy.18.trip_ref, f32[2,128,16,256]{3,2,1,0:T(8,128)} %echo_ref.3, s32[128,32]{1,0:T(8,128)} %bitcast.9), custom_call_target="tpu_custom_call" | custom-call | tf_op jit(solution)/shard_map/pallas_call | solution.py:157
  36.1 0.0 copy-start.1
  36.1 0.0 copy-start.2
  36.1 30.0 %shard_map.75.gram_ref = f32[96,128]{1,0:T(8,128)} custom-call(f32[3072,128]{1,0:T(8,128)} %bitcast.8), custom_call_target="tpu_custom_call" | custom-call | tf_op jit(solution)/shard_map/pallas_call | solution.py:231
  66.1 0.0 copy-done.3
  66.3 0.0 copy-done
  66.3 0.1 constant_dynamic-slice_fusion
  66.4 0.1 copy.16
  66.5 0.1 broadcast_multiply_fusion
  66.5 0.8 mul.43.right_ref
  67.3 7.6 %shard_map.76.own_ref = f32[8,128]{1,0:T(8,128)} custom-call(f32[96,128]{1,0:T(8,128)} %shard_map.75.gram_ref, f32[8,48,1]{2,1,0:T(8,128)} %mul.43.right_ref), custom_call_target="tpu_custom_call" | custom-call | tf_op jit(solution)/shard_map/pallas_call | solution.py:296
  75.0 11.1 %shard_map.77.weight_ref = f32[32,8,128]{2,1,0:T(8,128)} custom-call(f32[8,128]{1,0:T(8,128)} %shard_map.76.own_ref), custom_call_target="tpu_custom_call" | custom-call | tf_op jit(solution)/shard_map/pallas_call | solution.py:331
  86.1 10.3 %shard_map.78.power_ref = f32[128,256]{1,0:T(8,128)} custom-call(s32[128,3]{1,0:T(8,128)} %copy.18.trip_ref, f32[2,128,16,256]{3,2,1,0:T(8,128)} %echo_ref.3, f32[32,8,128]{2,1,0:T(8,128)} %shard_map.77.weight_ref), custom_call_target="tpu_custom_call" | custom-call | tf_op jit(solution)/shard_map/pallas_call | solution.py:376
  96.4 7.3 %shard_map.79.padded_ref = f32[64,768]{1,0:T(8,128)} custom-call(f32[128,256]{1,0:T(8,128)} %shard_map.78.power_ref), custom_call_target="tpu_custom_call" | custom-call | tf_op jit(solution)/shard_map/pallas_call | solution.py:484
  103.7 0.0 copy-done.1
  103.7 0.7 copy.19.guard_ref
  104.4 0.0 copy-done.2
  104.4 0.7 copy.20.train_ref
  105.1 3.7 %shard_map.80 = f32[64,512]{1,0:T(8,128)} custom-call(f32[64,768]{1,0:T(8,128)} %shard_map.79.padded_ref, s32[64,1]{1,0:T(8,128)} %copy.19.guard_ref, s32[64,1]{1,0:T(8,128)} %copy.20.train_ref), custom_call_target="tpu_custom_call" | custom-call | tf_op jit(solution)/shard_map/pallas_call | solution.py:546
  (2 shorter events, 0.1 us)
Async XLA Ops:
  0.0 66.3 %copy-start = (f32[128,3]{0,1:T(4,128)S(1)}, f32[128,3]{0,1:T(4,128)}, u32[]{:S(2)}) copy-start(f32[128,3]{0,1:T(4,128)} %param.9) | copy-start | bytes 4612
  0.0 66.1 %copy-start.3 = (f32[16]{0:T(128)S(1)}, f32[16]{0:T(128)}, u32[]{:S(2)}) copy-start(f32[16]{0:T(128)} %param.10) | copy-start | bytes 196
  36.1 67.6 %copy-start.1 = (s32[64]{0:T(128)S(1)}, s32[64]{0:T(128)}, u32[]{:S(2)}) copy-start(s32[64]{0:T(128)} %param.12) | copy-start | bytes 772
  36.1 68.3 %copy-start.2 = (s32[64]{0:T(128)S(1)}, s32[64]{0:T(128)}, u32[]{:S(2)}) copy-start(s32[64]{0:T(128)} %param.13) | copy-start | bytes 772

commit v2 on v1

--- a/solution.py
+++ b/solution.py
@@ -56,63 +56,66 @@
     pl.semaphore_wait(barrier, len(devices))
 
 
-def mask_kernel(dops, excl_ref, out_ref, send_sems, recv_sems, local_sem):
-    r = lax.axis_index("range")
-    y = lax.axis_index("dop")
-    greet([(r, (y + k) % dops) for k in range(1, dops)])
-    copies = []
-    for k in range(1, dops):
-        copies.append(
-            pltpu.make_async_remote_copy(
-                src_ref=excl_ref,
-                dst_ref=out_ref.at[y],
-                send_sem=send_sems.at[k - 1],
-                recv_sem=recv_sems.at[k - 1],
-                device_id=(r, (y + k) % dops),
-                device_id_type=MESH,
-            )
-        )
-        copies[-1].start()
-    own = pltpu.make_async_copy(excl_ref, out_ref.at[y], local_sem)
-    own.start()
-    own.wait()
-    for copy in copies:
-        copy.wait()
-
-
-def gather_mask(excluded, dops):
-    bins, blocks = excluded.shape
-    if dops == 1:
-        return excluded
-    gathered = pl.pallas_call(
-        functools.partial(mask_kernel, dops),
-        out_shape=jax.ShapeDtypeStruct((dops, bins, blocks), jnp.int32),
-        in_specs=[VMEM],
-        out_specs=VMEM,
-        scratch_shapes=[
-            pltpu.SemaphoreType.DMA((dops - 1,)),
-            pltpu.SemaphoreType.DMA((dops - 1,)),
-            pltpu.SemaphoreType.DMA,
-        ],
-        compiler_params=pltpu.CompilerParams(collective_id=0, has_side_effects=True),
-    )(excluded)
-    return gathered.reshape(dops * bins, blocks)
-
-
-def gram_kernel(trip_ref, echo_ref, excl_ref, out_ref, kept_ref):
+def stream_plan(sizes, pairs):
+    count = sizes[0] * sizes[1] * sizes[2] * sizes[3]
+    split_core = pairs % count == 0 and sizes[0] == 2
+    streams = pairs // count if split_core else pairs // (count // sizes[0])
+    return split_core, streams
+
+
+def gram_kernel(sizes, trip_ref, echo_ref, excl_ref, out_ref, *scratch):
+    (mask_ref, kept_ref, other_ref, from_core, own_ref, total_ref, recv_first, mid_ref,
+     recv_second, low_ref, recv_third, mask_send, mask_recv, send_sems, recv_sems) = scratch
+    core, dops, near, far = sizes
     slots = trip_ref.shape[1]
     chans, gates = echo_ref.shape[2:]
     span = slots * chans
     blocks = excl_ref.shape[1]
-    first = lax.axis_index("dop") * (gates // BLOCK)
+    split_core, streams = stream_plan(sizes, trip_ref.shape[0] // 2)
+    swap = 1 if streams > 1 and dops == near else 0
+    half = dops * near * far
+    block = half // dops
+    parts = my_parts(sizes)
+    c, y, x, z = parts
+
+    def device(axis, k):
+        moved = list(parts)
+        moved[axis] = (parts[axis] + k) % sizes[axis]
+        return place_of(sizes, chunk_index(sizes, moved))
+
+    greet([device(axis, k) for axis in range(4) for k in range(1, sizes[axis])])
+
+    def send(source, target, axis, k, sem, sends=send_sems, recvs=recv_sems):
+        copy = pltpu.make_async_remote_copy(
+            src_ref=source,
+            dst_ref=target,
+            send_sem=sends.at[sem],
+            recv_sem=recvs.at[sem],
+            device_id=device(axis, k),
+            device_id_type=MESH,
+        )
+        copy.start()
+        return copy
+
+    masks = [
+        send(excl_ref, mask_ref.at[y], 1, k, k - 1, mask_send, mask_recv)
+        for k in range(1, dops)
+    ]
+    mask_ref[y] = excl_ref[...]
     block_ids = lax.broadcasted_iota(jnp.int32, (blocks, gates), 0)
-    gate_blocks = lax.broadcasted_iota(jnp.int32, (blocks, gates), 1) // BLOCK + first
-    spread = jnp.where(block_ids == gate_blocks, 1.0, 0.0).astype(jnp.bfloat16)
-    kept_ref[...] = 1.0 - jnp.dot(
-        excl_ref[...].astype(jnp.float32).astype(jnp.bfloat16),
-        spread,
-        preferred_element_type=jnp.float32,
-    )
+    gate_blocks = lax.broadcasted_iota(jnp.int32, (blocks, gates), 1) // BLOCK
+    spread = jnp.where(
+        block_ids == gate_blocks + y * (gates // BLOCK), 1.0, 0.0
+    ).astype(jnp.bfloat16)
+    for copy in masks:
+        copy.wait()
+    for d in range(dops):
+        rows_here = excl_ref.shape[0]
+        kept_ref[d * rows_here : (d + 1) * rows_here, :] = 1.0 - jnp.dot(
+            mask_ref[d].astype(jnp.float32).astype(jnp.bfloat16),
+            spread,
+            preferred_element_type=jnp.float32,
+        )
     rows = lax.broadcasted_iota(jnp.int32, (span, LANES), 0)
     lanes = lax.broadcasted_iota(jnp.int32, (span, LANES), 1)
     upper_even = rows <= lanes
@@ -124,11 +127,18 @@
         high = values.astype(jnp.bfloat16)
         return high, (values - high.astype(jnp.float32)).astype(jnp.bfloat16)
 
-    def pair_step(pair, carry):
+    def pair_gram(which, s, pos):
+        q = pos // block
+        second = (pos // far) % near
+        turn = s * swap
+        at_y = q + turn * (second - q)
+        at_x = second + turn * (q - second)
+        owner = (which * dops + at_y) * near + at_x
+        pair = streams * (owner * far + pos % far) + s
         lefts = []
         rights = []
-        for s in range(2):
-            b = 2 * pair + s
+        for e in range(2):
+            b = 2 * pair + e
             u = jnp.concatenate([echo_ref[0, trip_ref[b, t]] for t in range(slots)], axis=0)
             v = jnp.concatenate([echo_ref[1, trip_ref[b, t]] for t in range(slots)], axis=0)
             kept = kept_ref[pl.ds(b, 1), :].astype(jnp.bfloat16)
@@ -145,103 +155,143 @@
         )
         even = jnp.where(upper_even, product[:span], product[span : 2 * span])
         odd = jnp.where(upper_odd, product[2 * span : 3 * span], product[3 * span :])
-        out_ref[pair] = jnp.where(is_even, even, odd)
-        return carry
-
-    lax.fori_loop(0, out_ref.shape[0], pair_step, 0)
-
-
-def gram(triplet, echoes, excl_all):
+        return jnp.where(is_even, even, odd)
+
+    which = c if split_core else 0
+    mine = [x if s * swap else y for s in range(streams)]
+    mine_first = mine[0]
+    mine_rest = mine[-1] if streams > 1 else mine[0]
+
+    def own_loop(first, count):
+        def step(i, carry):
+            s = i // (count * block)
+            j = i % (count * block)
+            me = mine_first + jnp.minimum(s, 1) * (mine_rest - mine_first)
+            pos = ((me + first + j // block) % dops) * block + j % block
+            own_ref[s * half + pos] = pair_gram(which, s, pos)
+            return carry
+
+        lax.fori_loop(0, streams * count * block, step, 0)
+
+    sem = 0
+    core_copy = None
+    if split_core:
+
+        def other_step(i, carry):
+            other_ref[i] = pair_gram((c + 1) % core, i // half, i % half)
+            return carry
+
+        lax.fori_loop(0, streams * half, other_step, 0)
+        core_copy = send(other_ref, from_core, 0, 1, sem)
+        sem += 1
+        own_loop(1, dops - 1)
+    else:
+        own_loop(1, dops)
+        if core == 2:
+            core_copy = send(own_ref, from_core, 0, 1, sem)
+            sem += 1
+    if core_copy is not None:
+        core_copy.wait()
+
+    def summed(s, q):
+        place = pl.ds(s * half + q * block, block)
+        value = own_ref[place]
+        return value + from_core[place] if core_copy is not None else value
+
+    copies = [[] for _ in range(streams)]
+    for s in range(streams):
+        for k in range(1, dops):
+            q = (mine[s] + k) % dops
+            total_ref[s, k - 1] = summed(s, q)
+            copies[s].append(
+                send(
+                    total_ref.at[s, k - 1],
+                    recv_first.at[s, k - 1],
+                    2 if s * swap else 1,
+                    k,
+                    sem,
+                )
+            )
+            sem += 1
+    if split_core:
+        own_loop(0, 1)
+    second_copies = [[] for _ in range(streams)]
+    for s in range(streams):
+        value = summed(s, mine[s])
+        for k in range(1, dops):
+            copies[s][k - 1].wait()
+            value = value + recv_first[s, k - 1]
+        mid_ref[s] = value
+        axis = 1 if s * swap else 2
+        for k in range(1, near):
+            q = (parts[axis] + k) % near
+            second_copies[s].append(
+                send(
+                    mid_ref.at[s, pl.ds(q * far, far)], recv_second.at[s, k - 1], axis, k, sem
+                )
+            )
+            sem += 1
+    third_copies = [[] for _ in range(streams)]
+    for s in range(streams):
+        axis = 1 if s * swap else 2
+        value = mid_ref[s, pl.ds(parts[axis] * far, far)]
+        for k in range(1, near):
+            second_copies[s][k - 1].wait()
+            value = value + recv_second[s, k - 1]
+        low_ref[s] = value
+        for k in range(1, far):
+            q = (z + k) % far
+            third_copies[s].append(
+                send(low_ref.at[s, q], recv_third.at[s, k - 1], 3, k, sem)
+            )
+            sem += 1
+    for s in range(streams):
+        value = low_ref[s, z]
+        for k in range(1, far):
+            third_copies[s][k - 1].wait()
+            value = value + recv_third[s, k - 1]
+        out_ref[s * span : (s + 1) * span, :] = value
+
+
+def reduced_grams(triplet, echoes, excluded, sizes):
     bins, slots = triplet.shape
     chans, gates = echoes.shape[2:]
+    span = slots * chans
+    core, dops, near, far = sizes
+    split_core, streams = stream_plan(sizes, bins // 2)
+    half = dops * near * far
+    block = half // dops
+    sends = (core - 1) + streams * ((dops - 1) + (near - 1) + (far - 1))
+
+    def buffer(*lead):
+        return pltpu.VMEM(tuple(max(n, 1) for n in lead) + (span, LANES), jnp.float32)
+
     return pl.pallas_call(
-        gram_kernel,
-        out_shape=jax.ShapeDtypeStruct((bins // 2, slots * chans, LANES), jnp.float32),
+        functools.partial(gram_kernel, sizes),
+        out_shape=jax.ShapeDtypeStruct((streams * span, LANES), jnp.float32),
         in_specs=[SMEM, VMEM, VMEM],
         out_specs=VMEM,
-        scratch_shapes=[pltpu.VMEM((bins, gates), jnp.float32)],
-        compiler_params=pltpu.CompilerParams(vmem_limit_bytes=VMEM_LIMIT),
-    )(triplet, echoes, excl_all)
-
-
-def reduce_plan(sizes, total_rows, span):
-    count = sizes[0] * sizes[1] * sizes[2] * sizes[3]
-    split_core = (total_rows // span) % count == 0
-    plan = []
-    rows = total_rows
-    for axis, group in enumerate(sizes):
-        if group == 1:
-            continue
-        after = rows if axis == 0 and not split_core else rows // group
-        plan.append((axis, group, rows, after))
-        rows = after
-    return plan, rows
-
-
-def reduce_kernel(sizes, plan, part_ref, out_ref, *scratch):
-    phases = len(plan)
-    recv_bufs = scratch[:phases]
-    sums = scratch[phases : 2 * phases - 1]
-    send_sems, recv_sems = scratch[2 * phases - 1 :]
-    parts = my_parts(sizes)
-
-    def peer(axis, group, k):
-        moved = list(parts)
-        moved[axis] = (parts[axis] + k) % group
-        return moved[axis], place_of(sizes, chunk_index(sizes, moved))
-
-    greet([peer(axis, group, k)[1] for axis, group, _, _ in plan for k in range(1, group)])
-    current = part_ref
-    sem = 0
-    for phase, (axis, group, before, after) in enumerate(plan):
-        whole = before == after
-        copies = []
-        for k in range(1, group):
-            where, device = peer(axis, group, k)
-            start = 0 if whole else pl.multiple_of(where * after, 8)
-            copies.append(
-                pltpu.make_async_remote_copy(
-                    src_ref=current.at[pl.ds(start, after)],
-                    dst_ref=recv_bufs[phase].at[k - 1],
-                    send_sem=send_sems.at[sem],
-                    recv_sem=recv_sems.at[sem],
-                    device_id=device,
-                    device_id_type=MESH,
-                )
-            )
-            copies[-1].start()
-            sem += 1
-        own = 0 if whole else pl.multiple_of(parts[axis] * after, 8)
-        for copy in copies:
-            copy.wait()
-        total = current[pl.ds(own, after), :]
-        for k in range(1, group):
-            total = total + recv_bufs[phase][k - 1]
-        if phase == phases - 1:
-            out_ref[...] = total
-        else:
-            sums[phase][...] = total
-            current = sums[phase]
-
-
-def reduce_grams(partial, sizes, span):
-    total_rows = partial.shape[0]
-    plan, rows = reduce_plan(sizes, total_rows, span)
-    copies = sum(group - 1 for _, group, _, _ in plan)
-    return pl.pallas_call(
-        functools.partial(reduce_kernel, sizes, plan),
-        out_shape=jax.ShapeDtypeStruct((rows, LANES), jnp.float32),
-        in_specs=[VMEM],
-        out_specs=VMEM,
         scratch_shapes=[
-            pltpu.VMEM((group - 1, after, LANES), jnp.float32) for _, group, _, after in plan
-        ]
-        + [pltpu.VMEM((after, LANES), jnp.float32) for _, _, _, after in plan[:-1]]
-        + [pltpu.SemaphoreType.DMA((copies,)), pltpu.SemaphoreType.DMA((copies,))],
+            pltpu.VMEM((dops,) + excluded.shape, jnp.int32),
+            pltpu.VMEM((bins, gates), jnp.float32),
+            buffer(streams * half if split_core else 1),
+            buffer(streams * half),
+            buffer(streams * half),
+            buffer(streams, dops - 1, block),
+            buffer(streams, dops - 1, block),
+            buffer(streams, block),
+            buffer(streams, near - 1, far),
+            buffer(streams, far),
+            buffer(streams, far - 1),
+            pltpu.SemaphoreType.DMA((max(dops - 1, 1),)),
+            pltpu.SemaphoreType.DMA((max(dops - 1, 1),)),
+            pltpu.SemaphoreType.DMA((max(sends, 1),)),
+            pltpu.SemaphoreType.DMA((max(sends, 1),)),
+        ],
         compiler_params=pltpu.CompilerParams(
             collective_id=1, has_side_effects=True, vmem_limit_bytes=VMEM_LIMIT
         ),
-    )(partial)
+    )(triplet, echoes, excluded)
 
 
 def solve_kernel(total_range, gram_ref, right_ref, out_ref):
@@ -366,7 +416,7 @@
             out_ref[pl.ds(b, 1), :] = yr * yr + yi * yi
         return carry
 
-    lax.fori_loop(0, owners, owner_step, 0)
+    lax.fori_loop(0, owners, owner_step, 0, unroll=4)
 
 
 def apply_weights(triplet, echoes, weights, owned):
@@ -559,8 +609,7 @@
     dops = lax.axis_size("dop")
     sizes = grid_sizes(ranges, dops)
     total_range = excluded.shape[1] * BLOCK * ranges
-    partial = gram(triplet, echoes, gather_mask(excluded, dops))
-    own_gram = reduce_grams(partial.reshape(bins // 2 * span, LANES), sizes, span)
+    own_gram = reduced_grams(triplet, echoes, excluded, sizes)
     owned = own_gram.shape[0] // span * 2
     owner = chunk_index(sizes, my_parts(sizes)) % (bins // owned)
     taper = lax.dynamic_slice_in_dim(bin_taper, owner * owned, owned, 0)

time: 109 us -> 90.6 us (0.83)
  Pallas kernels: 103 us -> 82.9 us
  local copies, waits for them, and re-layouts: 5.3 us -> 7.21 us
    pallas_call x3 -> x1, Pallas kernels: 63.3 us -> 45.2 us  [reduced_grams(): pl.pallas_call(functools.partial(gram_kernel, sizes), out_shape=jax.Shape...]
    pallas_call x1, Pallas kernels: 10.3 us -> 8.5 us  [apply_weights(): pl.pallas_call(functools.partial(power_kernel, owned), out_shape=jax.Shap...]
    unnamed x10 -> x4, local copies, waits for them, and re-layouts: 2.86 us -> 2.83 us
where the time goes in v2:
time: 90.6 us; the launch traced here: 90.3 us
  Pallas kernels  82.9 us (92%)
  local copies, waits for them, and re-layouts  7.21 us (8%)
    pallas_call x1, Pallas kernels, reduced_grams(): pl.pallas_call(functools.partial(gram_kernel, sizes), out_shape=jax.Shape...  45.2 us
    pallas_call x1, Pallas kernels, gather_weights(): pl.pallas_call(functools.partial(weights_kernel, sizes), out_shape=jax.Sh...  10.9 us
    pallas_call x1, Pallas kernels, apply_weights(): pl.pallas_call(functools.partial(power_kernel, owned), out_shape=jax.Shap...  8.5 us
    pallas_call x1, Pallas kernels, solve(): pl.pallas_call(functools.partial(solve_kernel, total_range), out_shape=ja...  7.61 us
    pallas_call x1, Pallas kernels, exchange_power(): pl.pallas_call(functools.partial(exchange_kernel, sizes), out_shape=jax.S...  7.13 us
    pallas_call x1, Pallas kernels, detect(): pl.pallas_call(functools.partial(detect_kernel, total_range), out_shape=j...  3.67 us
    unnamed x4, local copies, waits for them, and re-layouts  2.83 us

profile of v2, /device:TPU:0, one launch (start us, length us, event | category | flops | bytes accessed | tf_op | source)
XLA Modules:
  0.0 90.3 jit_solution(7603035516451918460)
XLA Ops:
  0.0 0.0 copy-start
  0.0 0.7 cosine_bitcast_fusion
  0.7 0.0 copy-done
  0.7 0.1 constant_dynamic-slice_fusion
  0.8 0.1 copy.16
  0.9 0.1 broadcast_multiply_fusion
  1.0 1.4 %copy.15.excl_ref = s32[64,32]{1,0:T(8,128)} copy(s32[64,32]{0,1:T(8,128)} %param.11) | data formatting | bytes 16384 | tf_op args[4]
  2.4 1.4 %copy.19.guard_ref = s32[64,1]{1,0:T(8,128)} copy(s32[64,1]{0,1:T(1,128)} %bitcast.6) | data formatting | bytes 512 | tf_op jit(solution)/shard_map/broadcast_in_dim | solution.py:601
  3.8 1.3 %copy.20.train_ref = s32[64,1]{1,0:T(8,128)} copy(s32[64,1]{0,1:T(1,128)} %bitcast.7) | data formatting | bytes 512 | tf_op jit(solution)/shard_map/broadcast_in_dim | solution.py:601
  5.1 1.4 %copy.18.trip_ref = s32[128,3]{1,0:T(8,128)} copy(s32[128,3]{0,1:T(4,128)} %param.8) | data formatting | bytes 3072 | tf_op args[1]
  6.5 45.2 %shard_map.73.gram_ref = f32[96,128]{1,0:T(8,128)} custom-call(s32[128,3]{1,0:T(8,128)} %copy.18.trip_ref, f32[2,128,16,256]{3,2,1,0:T(8,128)} %echo_ref.3, s32[64,32]{1,0:T(8,128)} %copy.15.excl_ref), custom_call_target="tpu_custom_call" | custom-call | tf_op jit(solution)/shard_map/pallas_call | solution.py:269
  51.7 0.8 mul.43.right_ref
  52.5 7.6 %shard_map.74.own_ref = f32[8,128]{1,0:T(8,128)} custom-call(f32[96,128]{1,0:T(8,128)} %shard_map.73.gram_ref, f32[8,48,1]{2,1,0:T(8,128)} %mul.43.right_ref), custom_call_target="tpu_custom_call" | custom-call | tf_op jit(solution)/shard_map/pallas_call | solution.py:346
  60.1 10.9 %shard_map.75.weight_ref = f32[32,8,128]{2,1,0:T(8,128)} custom-call(f32[8,128]{1,0:T(8,128)} %shard_map.74.own_ref), custom_call_target="tpu_custom_call" | custom-call | tf_op jit(solution)/shard_map/pallas_call | solution.py:381
  71.0 8.5 %shard_map.76.power_ref = f32[128,256]{1,0:T(8,128)} custom-call(s32[128,3]{1,0:T(8,128)} %copy.18.trip_ref, f32[2,128,16,256]{3,2,1,0:T(8,128)} %echo_ref.3, f32[32,8,128]{2,1,0:T(8,128)} %shard_map.75.weight_ref), custom_call_target="tpu_custom_call" | custom-call | tf_op jit(solution)/shard_map/pallas_call | solution.py:426
  79.5 7.1 %shard_map.77.padded_ref = f32[64,768]{1,0:T(8,128)} custom-call(f32[128,256]{1,0:T(8,128)} %shard_map.76.power_ref), custom_call_target="tpu_custom_call" | custom-call | tf_op jit(solution)/shard_map/pallas_call | solution.py:534
  86.6 3.7 %shard_map.78 = f32[64,512]{1,0:T(8,128)} custom-call(f32[64,768]{1,0:T(8,128)} %shard_map.77.padded_ref, s32[64,1]{1,0:T(8,128)} %copy.19.guard_ref, s32[64,1]{1,0:T(8,128)} %copy.20.train_ref), custom_call_target="tpu_custom_call" | custom-call | tf_op jit(solution)/shard_map/pallas_call | solution.py:596
  (1 shorter events, 0.0 us)
Async XLA Ops:
  0.0 0.7 copy-start

commit v3 on v2

--- a/solution.py
+++ b/solution.py
@@ -67,11 +67,11 @@
     (mask_ref, kept_ref, other_ref, from_core, own_ref, total_ref, recv_first, mid_ref,
      recv_second, low_ref, recv_third, mask_send, mask_recv, send_sems, recv_sems) = scratch
     core, dops, near, far = sizes
-    slots = trip_ref.shape[1]
+    slots = trip_ref.shape[0]
     chans, gates = echo_ref.shape[2:]
     span = slots * chans
-    blocks = excl_ref.shape[1]
-    split_core, streams = stream_plan(sizes, trip_ref.shape[0] // 2)
+    blocks = excl_ref.shape[0]
+    split_core, streams = stream_plan(sizes, trip_ref.shape[1] // 2)
     swap = 1 if streams > 1 and dops == near else 0
     half = dops * near * far
     block = half // dops
@@ -110,10 +110,11 @@
     for copy in masks:
         copy.wait()
     for d in range(dops):
-        rows_here = excl_ref.shape[0]
-        kept_ref[d * rows_here : (d + 1) * rows_here, :] = 1.0 - jnp.dot(
+        rows_here = excl_ref.shape[1]
+        kept_ref[d * rows_here : (d + 1) * rows_here, :] = 1.0 - lax.dot_general(
             mask_ref[d].astype(jnp.float32).astype(jnp.bfloat16),
             spread,
+            (((0,), (0,)), ((), ())),
             preferred_element_type=jnp.float32,
         )
     rows = lax.broadcasted_iota(jnp.int32, (span, LANES), 0)
@@ -139,8 +140,8 @@
         rights = []
         for e in range(2):
             b = 2 * pair + e
-            u = jnp.concatenate([echo_ref[0, trip_ref[b, t]] for t in range(slots)], axis=0)
-            v = jnp.concatenate([echo_ref[1, trip_ref[b, t]] for t in range(slots)], axis=0)
+            u = jnp.concatenate([echo_ref[0, trip_ref[t, b]] for t in range(slots)], axis=0)
+            v = jnp.concatenate([echo_ref[1, trip_ref[t, b]] for t in range(slots)], axis=0)
             kept = kept_ref[pl.ds(b, 1), :].astype(jnp.bfloat16)
             uh, ul = split(u)
             vh, vl = split(v)
@@ -171,7 +172,7 @@
             own_ref[s * half + pos] = pair_gram(which, s, pos)
             return carry
 
-        lax.fori_loop(0, streams * count * block, step, 0)
+        lax.fori_loop(0, streams * count * block, step, 0, unroll=2)
 
     sem = 0
     core_copy = None
@@ -181,7 +182,7 @@
             other_ref[i] = pair_gram((c + 1) % core, i // half, i % half)
             return carry
 
-        lax.fori_loop(0, streams * half, other_step, 0)
+        lax.fori_loop(0, streams * half, other_step, 0, unroll=2)
         core_copy = send(other_ref, from_core, 0, 1, sem)
         sem += 1
         own_loop(1, dops - 1)
@@ -272,7 +273,7 @@
         in_specs=[SMEM, VMEM, VMEM],
         out_specs=VMEM,
         scratch_shapes=[
-            pltpu.VMEM((dops,) + excluded.shape, jnp.int32),
+            pltpu.VMEM((dops,) + excluded.T.shape, jnp.int32),
             pltpu.VMEM((bins, gates), jnp.float32),
             buffer(streams * half if split_core else 1),
             buffer(streams * half),
@@ -291,7 +292,7 @@
         compiler_params=pltpu.CompilerParams(
             collective_id=1, has_side_effects=True, vmem_limit_bytes=VMEM_LIMIT
         ),
-    )(triplet, echoes, excluded)
+    )(triplet.T, echoes, excluded.T)
 
 
 def solve_kernel(total_range, gram_ref, right_ref, out_ref):
@@ -393,10 +394,10 @@
 
 
 def power_kernel(owned, trip_ref, echo_ref, weight_ref, out_ref, turned_ref):
-    slots = trip_ref.shape[1]
+    slots = trip_ref.shape[0]
     held = weight_ref.shape[1]
     span = turned_ref.shape[1]
-    owners = trip_ref.shape[0] // owned
+    owners = trip_ref.shape[1] // owned
     per_tile = LANES // held
     for tile in range(turned_ref.shape[0]):
         block = weight_ref[tile * per_tile : (tile + 1) * per_tile].reshape(LANES, LANES)
@@ -409,8 +410,8 @@
             b = owner * owned + k
             wr = rolled[:, 2 * k : 2 * k + 1]
             wi = rolled[:, 2 * k + 1 : 2 * k + 2]
-            u = jnp.concatenate([echo_ref[0, trip_ref[b, t]] for t in range(slots)], axis=0)
-            v = jnp.concatenate([echo_ref[1, trip_ref[b, t]] for t in range(slots)], axis=0)
+            u = jnp.concatenate([echo_ref[0, trip_ref[t, b]] for t in range(slots)], axis=0)
+            v = jnp.concatenate([echo_ref[1, trip_ref[t, b]] for t in range(slots)], axis=0)
             yr = jnp.sum(wr * u + wi * v, axis=0, keepdims=True)
             yi = jnp.sum(wr * v - wi * u, axis=0, keepdims=True)
             out_ref[pl.ds(b, 1), :] = yr * yr + yi * yi
@@ -430,7 +431,7 @@
         out_specs=VMEM,
         scratch_shapes=[pltpu.VMEM((tiles, slots * chans, LANES), jnp.float32)],
         compiler_params=pltpu.CompilerParams(vmem_limit_bytes=VMEM_LIMIT),
-    )(triplet, echoes, weights)
+    )(triplet.T, echoes, weights)
 
 
 def exchange_kernel(sizes, power_ref, out_ref, send_sems, recv_sems, local_sem):
@@ -549,8 +550,13 @@
     width = padded_ref.shape[1]
     cells = out_ref.shape[1]
     padded = padded_ref[...]
-    guard = guard_ref[...]
-    train = train_ref[...]
+
+    def column(ref):
+        row = jnp.broadcast_to(ref[...].astype(jnp.float32), (LANES, ref.shape[1]))
+        return row.T[:, :1].astype(jnp.int32)
+
+    guard = column(guard_ref)
+    train = column(train_ref)
 
     def ahead(values, by):
         return pltpu.roll(values, (width - by) % width, axis=1)
@@ -598,7 +604,7 @@
         out_shape=jax.ShapeDtypeStruct((bins, width - 2 * LANES), jnp.float32),
         in_specs=[VMEM, VMEM, VMEM],
         out_specs=VMEM,
-    )(padded, guard_len[:, None], train_len[:, None])
+    )(padded, guard_len[None, :], train_len[None, :])
 
 
 def shards(echoes, triplet, bin_taper, phases, excluded, guard_len, train_len):

time: 90.6 us -> 79.3 us (0.88)
  Pallas kernels: 82.9 us -> 77.3 us
  local copies, waits for them, and re-layouts: 7.21 us -> 1.69 us
    pallas_call x1, Pallas kernels: 45.2 us -> 39.5 us  [reduced_grams(): pl.pallas_call(functools.partial(gram_kernel, sizes), out_shape=jax.Shape...]
    unnamed x4 -> x2, local copies, waits for them, and re-layouts: 2.83 us -> 0.01 us
    broadcast_in_dim x2 -> x0, local copies, waits for them, and re-layouts: 2.7 us -> none  [the longest x1 1.35 us: detect(): guard_len[:, None]]
where the time goes in v3:
time: 79.3 us; the launch traced here: 79.1 us
  Pallas kernels  77.3 us (97%)
  local copies, waits for them, and re-layouts  1.69 us (2%)
    pallas_call x1, Pallas kernels, reduced_grams(): pl.pallas_call(functools.partial(gram_kernel, sizes), out_shape=jax.Shape...  39.5 us
    pallas_call x1, Pallas kernels, gather_weights(): pl.pallas_call(functools.partial(weights_kernel, sizes), out_shape=jax.Sh...  10.8 us
    pallas_call x1, Pallas kernels, apply_weights(): pl.pallas_call(functools.partial(power_kernel, owned), out_shape=jax.Shap...  8.49 us
    pallas_call x1, Pallas kernels, solve(): pl.pallas_call(functools.partial(solve_kernel, total_range), out_shape=ja...  7.61 us
    pallas_call x1, Pallas kernels, exchange_power(): pl.pallas_call(functools.partial(exchange_kernel, sizes), out_shape=jax.S...  7.13 us
    pallas_call x1, Pallas kernels, detect(): pl.pallas_call(functools.partial(detect_kernel, total_range), out_shape=j...  3.75 us

profile of v3, /device:TPU:0, one launch (start us, length us, event | category | flops | bytes accessed | tf_op | source)
XLA Modules:
  0.0 79.1 jit_solution(13375367247895400128)
XLA Ops:
  0.0 0.0 copy-start
  0.0 0.7 cosine_bitcast_fusion
  0.7 0.0 copy-done
  0.7 0.1 constant_dynamic-slice_fusion
  0.8 0.1 copy.9
  0.9 0.1 broadcast_multiply_fusion
  1.0 39.5 %shard_map.73.gram_ref = f32[96,128]{1,0:T(8,128)} custom-call(s32[3,128]{1,0:T(4,128)} %bitcast.9, f32[2,128,16,256]{3,2,1,0:T(8,128)} %echo_ref.3, s32[32,64]{1,0:T(8,128)} %bitcast.8), custom_call_target="tpu_custom_call" | custom-call | tf_op jit(solution)/shard_map/pallas_call | solution.py:270
  40.5 0.8 %mul.43.right_ref = f32[8,48,1]{2,1,0:T(8,128)} reshape(f32[4,2,3,16]{3,2,1,0:T(4,128)S(1)} %broadcast_multiply_fusion) | data formatting | bytes 3072 | tf_op jit(solution)/shard_map/mul | solution.py:623
  41.3 7.6 %shard_map.74.own_ref = f32[8,128]{1,0:T(8,128)} custom-call(f32[96,128]{1,0:T(8,128)} %shard_map.73.gram_ref, f32[8,48,1]{2,1,0:T(8,128)} %mul.43.right_ref), custom_call_target="tpu_custom_call" | custom-call | tf_op jit(solution)/shard_map/pallas_call | solution.py:347
  48.9 10.8 %shard_map.75.weight_ref = f32[32,8,128]{2,1,0:T(8,128)} custom-call(f32[8,128]{1,0:T(8,128)} %shard_map.74.own_ref), custom_call_target="tpu_custom_call" | custom-call | tf_op jit(solution)/shard_map/pallas_call | solution.py:382
  59.7 8.5 %shard_map.76.power_ref = f32[128,256]{1,0:T(8,128)} custom-call(s32[3,128]{1,0:T(4,128)} %bitcast.10, f32[2,128,16,256]{3,2,1,0:T(8,128)} %echo_ref.3, f32[32,8,128]{2,1,0:T(8,128)} %shard_map.75.weight_ref), custom_call_target="tpu_custom_call" | custom-call | tf_op jit(solution)/shard_map/pallas_call | solution.py:427
  68.2 7.1 %shard_map.77.padded_ref = f32[64,768]{1,0:T(8,128)} custom-call(f32[128,256]{1,0:T(8,128)} %shard_map.76.power_ref), custom_call_target="tpu_custom_call" | custom-call | tf_op jit(solution)/shard_map/pallas_call | solution.py:535
  75.4 3.7 %shard_map.78 = f32[64,512]{1,0:T(8,128)} custom-call(f32[64,768]{1,0:T(8,128)} %shard_map.77.padded_ref, s32[1,64]{1,0:T(1,128)} %bitcast.11, s32[1,64]{1,0:T(1,128)} %bitcast.12), custom_call_target="tpu_custom_call" | custom-call | tf_op jit(solution)/shard_map/pallas_call | solution.py:602
  (1 shorter events, 0.0 us)
Async XLA Ops:
  0.0 0.7 copy-start
